TPU v7x, 32 devices: a whole 2x2x4 slice. The times are simulated.
32 devices in a mesh: dev: 16 (over z, y, x), rep: 2 (over core).
Axes of the slice: x: 2, y: 2, z: 4, core: 2. Of those that a mesh axis runs over, the one named last changes fastest.
Arguments:
- tables: bfloat16 [64, 2048, 128], P('dev'), may hold values from -1.5 to 1.5
- bag_rows: int32 [32, 64, 32, 4], P(('rep', 'dev')), parts along dimension 0, may hold values from 0 to 2047
- bag_lengths: int32 [32, 64, 32], P(('rep', 'dev')), parts along dimension 0, may hold values from 1 to 4
- row_counts: int32 [32, 64], P(('rep', 'dev')), parts along dimension 0, may hold values from 1 to 32, as said below
- inverse: int32 [4096, 64], P(('rep', 'dev')), parts along dimension 0, may hold values from 0 to 31
- table_order: int32 [64], replicated, may hold values from 0 to 63, each once
- compress: bfloat16 [16, 64], replicated, may hold values from -0.75 to 0.75
- top_weight: bfloat16 [1024, 512], replicated, may hold values from -0.1875 to 0.1875
- top_bias: float32 [512], replicated, may hold values from -1.8 to 1.8
Outputs:
- ranked: bfloat16 [4096, 512], P(('rep', 'dev')), parts along dimension 0
There are 2 independent parts, one for each index of `rep`. A program takes and returns all parts, laid end to end along the dimension named above; an argument that names none is the same for every part. Nothing has to cross between parts.
Inputs may be any that keep to these rules, and one draw needn't show every extreme that they name: `row_counts`: for every sample device and every aligned group of 4 consecutive slots the counts sum to at most 80; a count of 32 and a group sum of 80 occur in every draw.
All inputs are finite; a program needn't handle non-finite values.
Results may differ from a plain program's by a relative error of at most 0.0062.
Values may be sent and summed in bfloat16 or wider, within the bound.
A program may use at most 128 MiB of HBM per device.

v0:
```python
import math

import jax
import jax.numpy as jnp
from jax import lax
from jax.sharding import PartitionSpec as P


def pool_bags(tables, bag_ids, bag_lens):
    vocabulary = tables.shape[1]
    table_rows = tables.reshape(-1, tables.shape[2])
    offsets = jnp.arange(tables.shape[0], dtype=jnp.int32) * vocabulary
    wanted = bag_ids + offsets[None, :, None, None]
    picked = jnp.take(table_rows, wanted, axis=0, mode="clip")
    places = jnp.arange(bag_ids.shape[3], dtype=jnp.int32)
    active = places[None, None, None, :] < bag_lens[..., None]
    summed = jnp.sum(jnp.where(active[..., None], picked.astype(jnp.float32), 0.0), axis=3)
    return summed.astype(jnp.bfloat16)


def shards(
    tables, bag_rows, bag_lengths, row_counts, inverse, table_order, compress, top_weight, top_bias
):
    width_emb = tables.shape[2]
    total_slots = table_order.shape[0]
    most_rows = bag_rows.shape[2]
    my_counts = row_counts[0]
    got_rows, got_lengths = (
        lax.all_to_all(bag_rows, "dev", split_axis=1, concat_axis=0, tiled=True),
        lax.all_to_all(bag_lengths, "dev", split_axis=1, concat_axis=0, tiled=True),
    )
    pooled = pool_bags(tables, got_rows, got_lengths)
    arrived = lax.all_to_all(pooled, "dev", split_axis=0, concat_axis=1, tiled=True).reshape(
        -1, width_emb
    )
    slot_base = jnp.arange(total_slots, dtype=jnp.int32) * most_rows
    slot_range = jnp.arange(total_slots, dtype=jnp.int32)
    matches = table_order[:, None] == slot_range[None, :]
    feature_base = jnp.sum(jnp.where(matches, slot_base[:, None], 0), axis=0)
    feature_count = jnp.sum(jnp.where(matches, my_counts[:, None], 0), axis=0)
    row_range = jnp.arange(most_rows, dtype=jnp.int32)
    feature_rows = jnp.take(
        arrived, feature_base[:, None] + row_range[None, :], axis=0, mode="clip"
    )
    samples = inverse.shape[0]
    block_rows = math.gcd(samples, 128)

    def score_block(inverse_block):
        present = inverse_block < feature_count[None, :]
        selector = (inverse_block[..., None] == row_range[None, None, :]) & present[..., None]
        selector = selector.astype(jnp.bfloat16)
        features = jnp.einsum(
            "bfu,fue->bfe", selector, feature_rows, preferred_element_type=jnp.float32
        ).astype(jnp.bfloat16)
        mixed = jnp.einsum(
            "kf,bfe->bke", compress, features, preferred_element_type=jnp.float32
        ).astype(jnp.bfloat16)
        pairwise = jnp.einsum(
            "bfe,bke->bfk", features, mixed, preferred_element_type=jnp.float32
        ).astype(jnp.bfloat16)
        hidden_pre = (
            jnp.dot(
                pairwise.reshape(pairwise.shape[0], -1),
                top_weight,
                preferred_element_type=jnp.float32,
            )
            + top_bias
        )
        return jnp.maximum(hidden_pre, 0.0).astype(jnp.bfloat16)

    ranked = lax.map(score_block, inverse.reshape(samples // block_rows, block_rows, total_slots))
    return ranked.reshape(samples, -1)


def solution(mesh):
    return jax.shard_map(
        shards,
        mesh=mesh,
        in_specs=(
            P("dev", None, None),
            P(("rep", "dev"), None, None, None),
            P(("rep", "dev"), None, None),
            P(("rep", "dev"), None),
            P(("rep", "dev"), None),
            P(),
            P(),
            P(),
            P(),
        ),
        out_specs=P(("rep", "dev"), None),
        check_vma=False,
    )
```

profile of v0, /device:TPU:0, one launch (start us, length us, event | category | flops | bytes accessed | tf_op | source)
XLA Modules:
  0.0 103.1 jit_solution(1663331126286047811)
XLA Ops:
  0.0 0.0 copy-start
  0.0 0.9 copy.24
  0.9 0.5 broadcast.69
  1.5 0.6 reduce.1
  2.1 0.7 reshape.111
  2.8 8.3 %all-to-all-start = ((s32[16,1,128]{2,1,0:T(1,128)}), s32[16,1,128]{2,1,0:T(1,128)S(1)}, u32[]{:S(2)}, u32[]{:S(2)}) async-start(s32[16,1,128]{2,1,0:T(1,128)} %reshape.111), calls=%async_computation | async-start | bytes 16384 | tf_op jit(solution)/shard_map/all_to_all | solution.py:30
  11.1 0.9 copy.25
  12.1 0.8 reshape.109
  12.9 5.6 %all-to-all-done = s32[16,1,128]{2,1,0:T(1,128)S(1)} async-done(((s32[16,1,128]{2,1,0:T(1,128)}), s32[16,1,128]{2,1,0:T(1,128)S(1)}, u32[]{:S(2)}, u32[]{:S(2)}) %all-to-all-start) | async-done | bytes 8224 | tf_op jit(solution)/shard_map/all_to_all | solution.py:30
  18.4 3.5 %all-to-all-start.1 = ((s32[16,1,512]{2,1,0:T(1,128)}), s32[16,1,512]{2,1,0:T(1,128)S(1)}, u32[]{:S(2)}, u32[]{:S(2)}) async-start(s32[16,1,512]{2,1,0:T(1,128)} %reshape.109), calls=%async_computation.1 | async-start | bytes 65536 | tf_op jit(solution)/shard_map/all_to_all | solution.py:29
  21.9 0.6 reduce.2
  22.5 0.1 reshape.112
  22.6 0.3 iota_compare_fusion.1
  23.0 6.3 %all-to-all-done.1 = s32[16,1,512]{2,1,0:T(1,128)S(1)} async-done(((s32[16,1,512]{2,1,0:T(1,128)}), s32[16,1,512]{2,1,0:T(1,128)S(1)}, u32[]{:S(2)}, u32[]{:S(2)}) %all-to-all-start.1) | async-done | bytes 32800 | tf_op jit(solution)/shard_map/all_to_all | solution.py:29
  29.3 0.6 reduce
  29.9 0.1 reshape.110
  30.1 0.1 broadcast_add_fusion
  30.2 0.5 copy.27
  30.6 0.6 reshape.91
  31.3 0.0 copy-done
  31.3 29.2 %gather_fusion = bf16[8192,128]{1,0:T(8,128)(2,1)} fusion(bf16[8192,128]{1,0:T(8,128)(2,1)S(1)} %bitcast.30, s32[8192]{0:T(1024)S(1)} %broadcast_clamp_fusion), kind=kCustom, calls=%fused_computation | custom fusion | bytes 4227072 | tf_op jit(solution)/shard_map/jit(_take)/gather | solution.py:14
  60.5 0.0 copy-start.4
  60.5 0.0 copy-start.5
  60.5 0.0 copy-start.1
  60.5 7.2 %fusion = bf16[16,4,32,128]{3,2,1,0:T(8,128)(2,1)} fusion(bf16[16,4,32,4,128]{4,3,2,1,0:T(4,128)(2,1)} %bitcast.32, pred[16,4,32,4]{3,2,1,0:T(8,128)(4,1)S(1)} %iota_compare_fusion.1), kind=kLoop, calls=%fused_computation.3 | loop fusion | flops 2883584 | bytes 2629632 | tf_op jit(solution)/shard_map/reduce_sum | solution.py:17
  67.7 3.6 %all-to-all-start.2 = ((bf16[16,4,32,128]{3,2,1,0:T(8,128)(2,1)}), bf16[16,4,32,128]{3,2,1,0:T(8,128)(2,1)S(1)}, u32[]{:S(2)}, u32[]{:S(2)}) async-start(bf16[16,4,32,128]{3,2,1,0:T(8,128)(2,1)} %fusion), calls=%async_computation.2 | async-start | bytes 1048576 | tf_op jit(solution)/shard_map/all_to_all | solution.py:33
  71.3 0.0 copy-done.4
  71.3 0.0 copy-done.5
  71.3 0.1 select_reduce_fusion
  71.4 0.1 iota_add_fusion
  71.5 0.1 reshape.99
  71.6 0.0 copy-done.1
  71.6 0.1 broadcast_compare_fusion
  71.7 12.4 %all-to-all-done.2 = bf16[16,4,32,128]{3,2,1,0:T(8,128)(2,1)S(1)} async-done(((bf16[16,4,32,128]{3,2,1,0:T(8,128)(2,1)}), bf16[16,4,32,128]{3,2,1,0:T(8,128)(2,1)S(1)}, u32[]{:S(2)}, u32[]{:S(2)}) %all-to-all-start.2) | async-done | bytes 524320 | tf_op jit(solution)/shard_map/all_to_all | solution.py:33
  84.1 6.2 %gather_fusion.1 = bf16[2048,128]{1,0:T(8,128)(2,1)S(1)} fusion(bf16[2048,128]{1,0:T(8,128)(2,1)S(1)} %bitcast.31, s32[2048]{0:T(1024)S(1)} %broadcast_clamp_fusion.1), kind=kCustom, calls=%fused_computation.1 | custom fusion | bytes 1056768 | tf_op jit(solution)/shard_map/jit(_take)/gather | solution.py:42
  90.3 2.1 %convert_bitcast_fusion = bf16[128,64,128]{0,2,1:T(8,128)(2,1)} fusion(bf16[64,32,128]{2,1,0:T(8,128)(2,1)S(1)} %bitcast.33, s32[128,64]{0,1:T(8,128)S(1)} %copy-done.1, pred[128,64]{0,1:T(8,128)(4,1)S(1)} %broadcast_compare_fusion), kind=kOutput, calls=%fused_computation.4 | convolution fusion | flops 68681728 | bytes 2662400 | tf_op jit(solution)/shard_map/while/body/eval_jaxpr/bfu,fue->bfe/dot_general | solution.py:52
  92.4 0.0 copy-start.2
  92.4 4.1 %copy.29 = bf16[128,64,128]{2,1,0:T(8,128)(2,1)} copy(bf16[128,64,128]{0,2,1:T(8,128)(2,1)} %convert_bitcast_fusion) | data formatting | bytes 4194304 | tf_op jit(solution)/shard_map/while/body/eval_jaxpr/convert_element_type | solution.py:54
  96.6 0.0 copy-done.2
  96.6 0.0 copy-start.3
  96.6 3.7 %convolution_convert_fusion = bf16[128,64,16]{1,2,0:T(8,128)(2,1)S(1)} fusion(bf16[128,64,128]{2,1,0:T(8,128)(2,1)} %copy.29, bf16[16,64]{1,0:T(8,128)(2,1)S(1)} %copy-done.2), kind=kOutput, calls=%fused_computation.5 | convolution fusion | flops 67502080 | bytes 2361344 | tf_op jit(solution)/shard_map/while/body/eval_jaxpr/bfe,bke->bfk/dot_general | solution.py:58
  100.3 0.6 copy.30
  100.9 0.0 copy-done.3
  100.9 2.2 %fusion.2 = bf16[128,512]{1,0:T(8,128)(2,1)} fusion(bf16[128,1024]{0,1:T(8,128)(2,1)S(1)} %bitcast.34, bf16[1024,512]{1,0:T(8,128)(2,1)} %param.16, f32[512]{0:T(512)S(1)} %copy-done.3), kind=kOutput, calls=%fused_computation.9 | convolution fusion | flops 134414336 | bytes 1443840 | tf_op jit(solution)/shard_map/while/body/eval_jaxpr/dot_general | solution.py:62
  (5 shorter events, 0.0 us)
Async XLA Ops:
  0.0 31.3 %copy-start = (bf16[4,2048,128]{2,1,0:T(8,128)(2,1)S(1)}, bf16[4,2048,128]{2,1,0:T(8,128)(2,1)}, u32[]{:S(2)}) copy-start(bf16[4,2048,128]{2,1,0:T(8,128)(2,1)} %param.9) | copy-start | bytes 6291460
  2.8 15.6 %all-to-all-start = ((s32[16,1,128]{2,1,0:T(1,128)}), s32[16,1,128]{2,1,0:T(1,128)S(1)}, u32[]{:S(2)}, u32[]{:S(2)}) async-start(s32[16,1,128]{2,1,0:T(1,128)} %reshape.111), calls=%async_computation | async-start | bytes 16384 | tf_op jit(solution)/shard_map/all_to_all | solution.py:30
  18.4 10.9 %all-to-all-start.1 = ((s32[16,1,512]{2,1,0:T(1,128)}), s32[16,1,512]{2,1,0:T(1,128)S(1)}, u32[]{:S(2)}, u32[]{:S(2)}) async-start(s32[16,1,512]{2,1,0:T(1,128)} %reshape.109), calls=%async_computation.1 | async-start | bytes 65536 | tf_op jit(solution)/shard_map/all_to_all | solution.py:29
  60.5 10.8 %copy-start.4 = (s32[1,64]{1,0:T(1,128)S(1)}, s32[1,64]{1,0:T(1,128)}, u32[]{:S(2)}) copy-start(s32[1,64]{1,0:T(1,128)} %param.12) | copy-start | bytes 772
  60.5 10.8 %copy-start.5 = (s32[64]{0:T(128)S(1)}, s32[64]{0:T(128)}, u32[]{:S(2)}) copy-start(s32[64]{0:T(128)} %param.14) | copy-start | bytes 772
  60.5 11.0 %copy-start.1 = (s32[128,64]{0,1:T(8,128)S(1)}, s32[128,64]{0,1:T(8,128)}, u32[]{:S(2)}) copy-start(s32[128,64]{0,1:T(8,128)} %param.13) | copy-start | bytes 98308
  67.7 16.4 %all-to-all-start.2 = ((bf16[16,4,32,128]{3,2,1,0:T(8,128)(2,1)}), bf16[16,4,32,128]{3,2,1,0:T(8,128)(2,1)S(1)}, u32[]{:S(2)}, u32[]{:S(2)}) async-start(bf16[16,4,32,128]{3,2,1,0:T(8,128)(2,1)} %fusion), calls=%async_computation.2 | async-start | bytes 1048576 | tf_op jit(solution)/shard_map/all_to_all | solution.py:33
  92.4 4.2 %copy-start.2 = (bf16[16,64]{1,0:T(8,128)(2,1)S(1)}, bf16[16,64]{1,0:T(8,128)(2,1)}, u32[]{:S(2)}) copy-start(bf16[16,64]{1,0:T(8,128)(2,1)} %param.15) | copy-start | bytes 6148
  96.6 4.3 %copy-start.3 = (f32[512]{0:T(512)S(1)}, f32[512]{0:T(512)}, u32[]{:S(2)}) copy-start(f32[512]{0:T(512)} %param.17) | copy-start | bytes 6148
where the time goes:
time: 104 us; the launch traced here: 103 us
  local copies, waits for them, and re-layouts  45.4 us (44%)
  waiting for transfers between devices  24.3 us (23%)
  starting transfers between devices  15.4 us (15%)
  other arithmetic  9.72 us (9%)
  matrix products  8.03 us (8%)
    gather x1, local copies, waits for them, and re-layouts, pool_bags(): picked = jnp.take(table_rows, wanted, axis=0, mode='clip')  29.2 us
    all_to_all x1, waiting for transfers between devices, shards(): lax.all_to_all(pooled, 'dev', split_axis=0, concat_axis=1, tiled=True)  12.4 us
    all_to_all x1, starting transfers between devices, shards(): lax.all_to_all(bag_lengths, 'dev', split_axis=1, concat_axis=0, tiled=True)  8.34 us
    reduce_sum x1, other arithmetic, pool_bags(): jnp.sum(jnp.where(active[..., None], picked.astype(jnp.float32), 0.0), ax...  7.16 us
    all_to_all x1, waiting for transfers between devices, shards(): lax.all_to_all(bag_rows, 'dev', split_axis=1, concat_axis=0, tiled=True)  6.33 us
    gather x1, local copies, waits for them, and re-layouts, shards(): jnp.take(arrived, feature_base[:, None] + row_range[None, :], axis=0, mod...  6.17 us
    all_to_all x1, waiting for transfers between devices, shards(): lax.all_to_all(bag_lengths, 'dev', split_axis=1, concat_axis=0, tiled=True)  5.57 us
    convert_element_type x1, local copies, waits for them, and re-layouts, score_block(): features = jnp.einsum('bfu,fue->bfe', selector, feature_rows, preferred_e...  4.15 us
  transfers between devices with their start and end apart: 3, of which 3 were waited for; matrix products, arithmetic and copies ran while one was open for 3% of the time, Pallas kernels for 0%

commit v1 on v0

v1 whole, which is shorter than its diff:
```python
import functools

import jax
import jax.numpy as jnp
from jax import lax
from jax.experimental import pallas as pl
from jax.experimental.pallas import tpu as pltpu
from jax.sharding import PartitionSpec as P

F32 = jnp.float32
BF16 = jnp.bfloat16


def exchange_kernel(
    n, most, bags_ref, tables_ref, rows_ref,
    tab16, tab32, ids_out, ids_vm, ids_in, pooled, staging,
    tab_sem, id_send, id_recv, smem_sem, row_send, row_recv, own_sem,
):
    me = lax.axis_index("dev")
    tabs, vocab, width = tables_ref.shape
    spread = bags_ref.shape[0]
    pooling = spread // most
    zero_row = tabs * vocab

    table_copy = pltpu.make_async_copy(tables_ref, tab16, tab_sem)
    table_copy.start()
    barrier = pltpu.get_barrier_semaphore()

    def greet(i, carry):
        pl.semaphore_signal(barrier, inc=1, device_id={"dev": lax.rem(me + i, n)})
        return carry

    lax.fori_loop(1, n, greet, 0)

    index = bags_ref[...].T
    for g in range(n):
        ids_out[g] = index[g * tabs:(g + 1) * tabs]

    pl.semaphore_wait(barrier, n - 1)

    def id_copy(i):
        peer = lax.rem(me + i, n)
        return pltpu.make_async_remote_copy(
            src_ref=ids_out.at[peer], dst_ref=ids_vm.at[me],
            send_sem=id_send.at[peer], recv_sem=id_recv.at[me],
            device_id={"dev": peer},
        )

    def id_arrival(source):
        return pltpu.make_async_remote_copy(
            src_ref=ids_out.at[source], dst_ref=ids_vm.at[source],
            send_sem=id_send.at[source], recv_sem=id_recv.at[source],
            device_id={"dev": source},
        )

    def offset(j):
        half = (j + 1) // 2
        return n // 2 + jnp.where(j % 2 == 1, half, -half)

    def send_ids(j, carry):
        id_copy(offset(j)).start()
        return carry

    lax.fori_loop(0, n - 1, send_ids, 0)

    table_copy.wait()
    tab32[pl.ds(zero_row, 8), :] = jnp.zeros((8, width), F32)
    step = 256

    def widen(i, carry):
        for t in range(tabs):
            base = pl.multiple_of(i * step, step)
            tab32[pl.ds(t * vocab + base, step), :] = tab16[t, pl.ds(base, step), :].astype(F32)
        return carry

    lax.fori_loop(0, vocab // step, widen, 0)

    def pool(source_ref, store):
        def eight(i, carry):
            for t in range(tabs):
                parts = []
                for r in range(8):
                    total = None
                    for p in range(pooling):
                        at = source_ref[t, (i * 8 + r) * pooling + p]
                        row = tab32[pl.ds(at, 1), :]
                        total = row if total is None else total + row
                    pooled[pl.ds(t * most + i * 8 + r, 1), :] = total
            return carry

        lax.fori_loop(0, most // 8, eight, 0)
        store(pooled[...].astype(BF16))

    def row_copy(peer):
        return pltpu.make_async_remote_copy(
            src_ref=staging.at[peer], dst_ref=rows_ref.at[me],
            send_sem=row_send.at[peer], recv_sem=row_recv.at[me],
            device_id={"dev": peer},
        )

    def serve(j, carry):
        peer = lax.rem(me + offset(j), n)
        id_arrival(peer).wait_recv()
        down = pltpu.make_async_copy(ids_vm.at[peer], ids_in, smem_sem)
        down.start()
        down.wait()

        def store(value):
            staging[peer] = value

        pool(ids_in, store)
        row_copy(peer).start()
        return carry

    lax.fori_loop(0, n - 1, serve, 0)

    down = pltpu.make_async_copy(ids_out.at[me], ids_in, smem_sem)
    down.start()
    down.wait()

    def store_own(value):
        rows_ref[me] = value

    pool(ids_in, store_own)

    def finish(i, carry):
        peer = lax.rem(me + i, n)
        id_copy(i).wait_send()
        row_copy(peer).wait_send()
        pltpu.make_async_remote_copy(
            src_ref=staging.at[peer], dst_ref=rows_ref.at[peer],
            send_sem=row_send.at[peer], recv_sem=row_recv.at[peer],
            device_id={"dev": peer},
        ).wait_recv()
        return carry

    lax.fori_loop(1, n, finish, 0)


def exchange(n, most, bags, tables):
    tabs, vocab, width = tables.shape
    spread, slots = bags.shape
    block = tabs * most
    vmem = pl.BlockSpec(memory_space=pltpu.VMEM)
    return pl.pallas_call(
        functools.partial(exchange_kernel, n, most),
        out_shape=jax.ShapeDtypeStruct((n, block, width), BF16),
        in_specs=[vmem, pl.BlockSpec(memory_space=pl.ANY)],
        out_specs=vmem,
        scratch_shapes=[
            pltpu.VMEM(tables.shape, BF16),
            pltpu.VMEM((tabs * vocab + 8, width), F32),
            pltpu.VMEM((n, tabs, spread), jnp.int32),
            pltpu.VMEM((n, tabs, spread), jnp.int32),
            pltpu.SMEM((tabs, spread), jnp.int32),
            pltpu.VMEM((block, width), F32),
            pltpu.VMEM((n, block, width), BF16),
            pltpu.SemaphoreType.DMA,
            pltpu.SemaphoreType.DMA((n,)),
            pltpu.SemaphoreType.DMA((n,)),
            pltpu.SemaphoreType.DMA,
            pltpu.SemaphoreType.DMA((n,)),
            pltpu.SemaphoreType.DMA((n,)),
            pltpu.SemaphoreType.DMA,
        ],
        compiler_params=pltpu.CompilerParams(
            collective_id=0, has_side_effects=True, vmem_limit_bytes=48 << 20
        ),
        name="exchange",
    )(bags, tables)


def interact_kernel(
    rows_ref, inv_ref, order_ref, counts_ref, compress_ref, weight_ref, bias_ref, out_ref,
    sel, spread_c, mask, mixed, pairs,
):
    features, samples = inv_ref.shape
    mixes = compress_ref.shape[0]
    total, width = rows_ref.shape
    most = total // features
    per = 8
    span = per * most
    inv = inv_ref[...].astype(F32).T.astype(BF16)
    comp = compress_ref[...]

    def select(c, carry):
        lane = lax.broadcasted_iota(jnp.int32, (1, span), 1)
        slot, unit = lane // most, lane % most
        order_row = jnp.zeros((1, span), jnp.int32)
        count_row = jnp.zeros((1, span), jnp.int32)
        row_u = lax.broadcasted_iota(jnp.int32, (most, samples), 0)
        for i in range(per):
            s = c * per + i
            f, count = order_ref[s], counts_ref[s]
            order_row = jnp.where(slot == i, f, order_row)
            count_row = jnp.where(slot == i, count, count_row)
            wanted = inv_ref[pl.ds(f, 1), :]
            hit = jnp.logical_and(row_u == wanted, row_u < count)
            mask[pl.ds(pl.multiple_of(s * most, most), most), :] = jnp.where(hit, 1.0, 0.0)
        target = jnp.where(unit < count_row, unit, -1).astype(F32)
        feature = lax.broadcasted_iota(jnp.int32, (features, span), 0)
        one_hot = jnp.where(feature == order_row, 1.0, 0.0).astype(BF16)
        inv_all = jnp.dot(inv, one_hot, preferred_element_type=F32)
        columns = pl.ds(pl.multiple_of(c * span, span), span)
        sel[:, columns] = jnp.where(inv_all == target, 1.0, 0.0).astype(BF16)
        spread_c[:, columns] = jnp.dot(comp, one_hot, preferred_element_type=F32)
        return carry

    lax.fori_loop(0, features // per, select, 0)

    deep = min(total, 2048)

    def mix(k, carry):
        acc = jnp.zeros((samples, width), F32)

        def part(q, acc):
            columns = pl.ds(pl.multiple_of(q * deep, deep), deep)
            scaled = sel[:, columns] * spread_c[pl.ds(k, 1), columns].astype(BF16)
            return acc + jnp.dot(scaled, rows_ref[columns, :], preferred_element_type=F32)

        if total == deep:
            acc = part(0, acc)
        else:
            acc = lax.fori_loop(0, total // deep, part, acc)
        mixed[pl.ds(pl.multiple_of(k * samples, samples), samples), :] = acc.astype(BF16)
        return carry

    lax.fori_loop(0, mixes, mix, 0)

    pair = 2

    def inner(j, carry):
        c8, kp = j // (mixes // pair), j % (mixes // pair)
        wanted = mixed[pl.ds(pl.multiple_of(kp * pair * samples, samples), pair * samples), :]
        for i in range(per):
            c = c8 * per + i
            at = pl.ds(pl.multiple_of(c * span, span), span)
            product = lax.dot_general(
                rows_ref[at, :], wanted, (((1,), (1,)), ((), ())), preferred_element_type=F32
            )
            chosen = mask[at, :]
            for h in range(pair):
                kept = product[:, h * samples:(h + 1) * samples] * chosen
                summed = jnp.sum(kept.reshape(per, most, samples), axis=1)
                for s in range(per):
                    f = order_ref[c * per + s]
                    pairs[pl.ds(f * mixes + kp * pair + h, 1), :] = summed[s:s + 1, :]
        return carry

    lax.fori_loop(0, features // (per * per) * (mixes // pair), inner, 0)

    depth = min(features * mixes, 1024)
    hidden = jnp.zeros(out_ref.shape, F32) + bias_ref[...]

    def top(q, hidden):
        at = pl.ds(pl.multiple_of(q * depth, depth), depth)
        return hidden + lax.dot_general(
            pairs[at, :].astype(BF16), weight_ref[at, :], (((0,), (0,)), ((), ())),
            preferred_element_type=F32,
        )

    if depth == features * mixes:
        hidden = top(0, hidden)
    else:
        hidden = lax.fori_loop(0, features * mixes // depth, top, hidden)
    out_ref[...] = jnp.maximum(hidden, 0.0).astype(BF16)


def interact(rows, inv, order, counts, compress, weight, bias):
    features, samples = inv.shape
    mixes = compress.shape[0]
    total, width = rows.shape
    vmem = pl.BlockSpec(memory_space=pltpu.VMEM)
    smem = pl.BlockSpec(memory_space=pltpu.SMEM)
    return pl.pallas_call(
        interact_kernel,
        out_shape=jax.ShapeDtypeStruct((samples, weight.shape[1]), BF16),
        in_specs=[vmem, vmem, smem, smem, vmem, vmem, vmem],
        out_specs=vmem,
        scratch_shapes=[
            pltpu.VMEM((samples, total), BF16),
            pltpu.VMEM((mixes, total), F32),
            pltpu.VMEM((total, samples), F32),
            pltpu.VMEM((mixes * samples, width), BF16),
            pltpu.VMEM((features * mixes, samples), F32),
        ],
        compiler_params=pltpu.CompilerParams(vmem_limit_bytes=60 << 20),
        name="interact",
    )(rows, inv, order, counts, compress, weight, bias)


def shards(
    n, tables, bag_rows, bag_lengths, row_counts, inverse, table_order, compress, top_weight, top_bias
):
    _, slots, most, pooling = bag_rows.shape
    tabs, vocab, width = tables.shape
    local = (jnp.arange(slots, dtype=jnp.int32) % tabs) * vocab
    active = jnp.arange(pooling, dtype=jnp.int32)[:, None] < bag_lengths[0].T[:, None, :]
    index = jnp.where(active, bag_rows[0].transpose(1, 2, 0) + local, tabs * vocab)
    rows = exchange(n, most, index.reshape(most * pooling, slots), tables)
    return interact(
        rows.reshape(slots * most, width), inverse.T, table_order, row_counts[0],
        compress, top_weight, top_bias.reshape(1, -1),
    )


def solution(mesh):
    return jax.shard_map(
        functools.partial(shards, mesh.shape["dev"]),
        mesh=mesh,
        in_specs=(
            P("dev", None, None),
            P(("rep", "dev"), None, None, None),
            P(("rep", "dev"), None, None),
            P(("rep", "dev"), None),
            P(("rep", "dev"), None),
            P(),
            P(),
            P(),
            P(),
        ),
        out_specs=P(("rep", "dev"), None),
        check_vma=False,
    )
```

time: 104 us -> 52.4 us (0.50)
  Pallas kernels: 0 us -> 48.9 us
  local copies, waits for them, and re-layouts: 45.4 us -> 2.36 us
  waiting for transfers between devices: 24.3 us -> 0 us
  starting transfers between devices: 15.4 us -> 0 us
  other arithmetic: 9.72 us -> 0.87 us
  matrix products: 8.03 us -> 0 us
    pallas_call x0 -> x2, Pallas kernels: none -> 48.9 us  [the longest x1 35.9 us: exchange(): pl.pallas_call(functools.partial(exchange_kernel, n, most), out_shape=jax...]
    gather x2 -> x0, local copies, waits for them, and re-layouts: 35.4 us -> none  [the longest x1 29.2 us: pool_bags(): picked = jnp.take(table_rows, wanted, axis=0, mode='clip')]
    all_to_all x3 -> x0, waiting for transfers between devices: 24.3 us -> none  [the longest x1 12.4 us: shards(): lax.all_to_all(pooled, 'dev', split_axis=0, concat_axis=1, tiled=True)]
    all_to_all x3 -> x0, starting transfers between devices: 15.4 us -> none  [the longest x1 8.34 us: shards(): lax.all_to_all(bag_lengths, 'dev', split_axis=1, concat_axis=0, tiled=True)]
    dot_general x3 -> x0, matrix products: 8.03 us -> none  [the longest x1 3.7 us: score_block(): jnp.einsum('bfe,bke->bfk', features, mixed, preferred_element_type=jnp.fl...]
    reduce_sum x2 -> x0, other arithmetic: 7.27 us -> none  [the longest x1 7.16 us: pool_bags(): jnp.sum(jnp.where(active[..., None], picked.astype(jnp.float32), 0.0), ax...]
    convert_element_type x2 -> x0, local copies, waits for them, and re-layouts: 4.75 us -> none  [the longest x1 4.15 us: score_block(): features = jnp.einsum('bfu,fue->bfe', selector, feature_rows, preferred_e...]
    all_to_all x2 -> x0, other arithmetic: 1.21 us -> none  [the longest x1 0.63 us: shards(): lax.all_to_all(bag_rows, 'dev', split_axis=1, concat_axis=0, tiled=True)]
  transfers between devices with their start and end apart: 3 -> 0, of which waited for: 3 -> 0; matrix products, arithmetic and copies ran while one was open for 3% -> 0% of each run, Pallas kernels for 0% -> 0%
where the time goes in v1:
time: 52.4 us; the launch traced here: 52.2 us
  Pallas kernels  48.9 us (93%)
  local copies, waits for them, and re-layouts  2.36 us (5%)
  other arithmetic  0.87 us (2%)
    pallas_call x1, Pallas kernels, exchange(): pl.pallas_call(functools.partial(exchange_kernel, n, most), out_shape=jax...  35.9 us
    pallas_call x1, Pallas kernels, interact(): pl.pallas_call(interact_kernel, out_shape=jax.ShapeDtypeStruct((samples,...  13 us
    unnamed x4, local copies, waits for them, and re-layouts  2.36 us

profile of v1, /device:TPU:0, one launch (start us, length us, event | category | flops | bytes accessed | tf_op | source)
XLA Modules:
  0.0 52.2 jit_solution(18254115679798382286)
XLA Ops:
  0.0 0.9 %bitcast_select_fusion = s32[32,4,64]{2,1,0:T(4,128)S(1)} fusion(s32[1,64,32,4]{1,3,2,0:T(4,128)} %param.10, s32[64]{0:T(128)S(1)} %fusion, s32[32,64]{1,0:T(8,128)} %bitcast.17), kind=kLoop, calls=%fused_computation | loop fusion | flops 24576 | bytes 73984 | tf_op jit(solution)/shard_map/jit(_where)/select_n | solution.py:299
  0.9 0.0 copy-start
  0.9 1.6 %copy-done = bf16[4,2048,128]{2,1,0:T(8,128)(2,1)S(1)} copy-done((bf16[4,2048,128]{2,1,0:T(8,128)(2,1)S(1)}, bf16[4,2048,128]{2,1,0:T(8,128)(2,1)}, u32[]{:S(2)}) %copy-start) | copy-done | bytes 2097176
  2.5 35.9 %exchange.1 = bf16[16,128,128]{2,1,0:T(8,128)(2,1)S(1)} custom-call(s32[128,64]{1,0:T(8,128)S(1)} %bitcast.15, bf16[4,2048,128]{2,1,0:T(8,128)(2,1)S(1)} %copy-done), custom_call_target="tpu_custom_call" | custom-call | tf_op jit(solution)/shard_map/exchange/pallas_call | solution.py:145
  38.4 0.0 copy-start.1
  38.4 0.8 %copy-done.1 = bf16[16,128,128]{2,1,0:T(8,128)(2,1)} copy-done((bf16[16,128,128]{2,1,0:T(8,128)(2,1)}, bf16[16,128,128]{2,1,0:T(8,128)(2,1)S(1)}, u32[]{:S(2)}) %copy-start.1) | copy-done | bytes 524312
  39.2 13.0 %interact.1 = bf16[128,512]{1,0:T(8,128)(2,1)} custom-call(bf16[2048,128]{1,0:T(8,128)(2,1)} %bitcast.14, s32[64,128]{1,0:T(8,128)} %bitcast.16, s32[64]{0:T(128)} %order_ref.1, s32[64]{0:T(128)} %bitcast.19, bf16[16,64]{1,0:T(8,128)(2,1)} %compress_ref.1, bf16[1024,512]{1,0:T(8,128)(2,1)} %weight_ref.1, f32[1,512]{1,0:T(1,128)} %bitcast.18), custom_call_target="tpu_custom_call" | custom-call | tf_op jit(solution)/shard_map/interact/pallas_call | solution.py:275
  (1 shorter events, 0.0 us)
Async XLA Ops:
  0.9 1.6 %copy-start = (bf16[4,2048,128]{2,1,0:T(8,128)(2,1)S(1)}, bf16[4,2048,128]{2,1,0:T(8,128)(2,1)}, u32[]{:S(2)}) copy-start(bf16[4,2048,128]{2,1,0:T(8,128)(2,1)} %tables_ref.1) | copy-start | bytes 6291460
  38.4 0.8 %copy-start.1 = (bf16[16,128,128]{2,1,0:T(8,128)(2,1)}, bf16[16,128,128]{2,1,0:T(8,128)(2,1)S(1)}, u32[]{:S(2)}) copy-start(bf16[16,128,128]{2,1,0:T(8,128)(2,1)S(1)} %exchange.1) | copy-start | bytes 1572868

commit v2 on v1

--- a/solution.py
+++ b/solution.py
@@ -13,8 +13,8 @@
 
 def exchange_kernel(
     n, most, bags_ref, tables_ref, rows_ref,
-    tab16, tab32, ids_out, ids_vm, ids_in, pooled, staging,
-    tab_sem, id_send, id_recv, smem_sem, row_send, row_recv, own_sem,
+    tab16, tab32, ids_out, ids_in, pooled, staging,
+    tab_sem, id_send, id_recv, smem_sem, row_send, row_recv,
 ):
     me = lax.axis_index("dev")
     tabs, vocab, width = tables_ref.shape
@@ -41,14 +41,14 @@
     def id_copy(i):
         peer = lax.rem(me + i, n)
         return pltpu.make_async_remote_copy(
-            src_ref=ids_out.at[peer], dst_ref=ids_vm.at[me],
+            src_ref=ids_out.at[peer], dst_ref=ids_in.at[me],
             send_sem=id_send.at[peer], recv_sem=id_recv.at[me],
             device_id={"dev": peer},
         )
 
     def id_arrival(source):
         return pltpu.make_async_remote_copy(
-            src_ref=ids_out.at[source], dst_ref=ids_vm.at[source],
+            src_ref=ids_out.at[source], dst_ref=ids_in.at[source],
             send_sem=id_send.at[source], recv_sem=id_recv.at[source],
             device_id={"dev": source},
         )
@@ -63,6 +63,8 @@
 
     lax.fori_loop(0, n - 1, send_ids, 0)
 
+    own_ids = pltpu.make_async_copy(ids_out.at[me], ids_in.at[me], smem_sem)
+    own_ids.start()
     table_copy.wait()
     tab32[pl.ds(zero_row, 8), :] = jnp.zeros((8, width), F32)
     step = 256
@@ -75,20 +77,18 @@
 
     lax.fori_loop(0, vocab // step, widen, 0)
 
-    def pool(source_ref, store):
-        def eight(i, carry):
-            for t in range(tabs):
-                parts = []
-                for r in range(8):
-                    total = None
-                    for p in range(pooling):
-                        at = source_ref[t, (i * 8 + r) * pooling + p]
-                        row = tab32[pl.ds(at, 1), :]
-                        total = row if total is None else total + row
-                    pooled[pl.ds(t * most + i * 8 + r, 1), :] = total
+    def pool(source, store):
+        def one_table(t, carry):
+            at_table = pl.multiple_of(t * most, most)
+            for r in range(most):
+                total = None
+                for p in range(pooling):
+                    row = tab32[pl.ds(ids_in[source, t, r * pooling + p], 1), :]
+                    total = row if total is None else total + row
+                pooled[pl.ds(at_table + r, 1), :] = total
             return carry
 
-        lax.fori_loop(0, most // 8, eight, 0)
+        lax.fori_loop(0, tabs, one_table, 0)
         store(pooled[...].astype(BF16))
 
     def row_copy(peer):
@@ -101,27 +101,22 @@
     def serve(j, carry):
         peer = lax.rem(me + offset(j), n)
         id_arrival(peer).wait_recv()
-        down = pltpu.make_async_copy(ids_vm.at[peer], ids_in, smem_sem)
-        down.start()
-        down.wait()
 
         def store(value):
             staging[peer] = value
 
-        pool(ids_in, store)
+        pool(peer, store)
         row_copy(peer).start()
         return carry
 
     lax.fori_loop(0, n - 1, serve, 0)
 
-    down = pltpu.make_async_copy(ids_out.at[me], ids_in, smem_sem)
-    down.start()
-    down.wait()
+    own_ids.wait()
 
     def store_own(value):
         rows_ref[me] = value
 
-    pool(ids_in, store_own)
+    pool(me, store_own)
 
     def finish(i, carry):
         peer = lax.rem(me + i, n)
@@ -151,8 +146,7 @@
             pltpu.VMEM(tables.shape, BF16),
             pltpu.VMEM((tabs * vocab + 8, width), F32),
             pltpu.VMEM((n, tabs, spread), jnp.int32),
-            pltpu.VMEM((n, tabs, spread), jnp.int32),
-            pltpu.SMEM((tabs, spread), jnp.int32),
+            pltpu.SMEM((n, tabs, spread), jnp.int32),
             pltpu.VMEM((block, width), F32),
             pltpu.VMEM((n, block, width), BF16),
             pltpu.SemaphoreType.DMA,
@@ -161,10 +155,9 @@
             pltpu.SemaphoreType.DMA,
             pltpu.SemaphoreType.DMA((n,)),
             pltpu.SemaphoreType.DMA((n,)),
-            pltpu.SemaphoreType.DMA,
         ],
         compiler_params=pltpu.CompilerParams(
-            collective_id=0, has_side_effects=True, vmem_limit_bytes=48 << 20
+            collective_id=0, has_side_effects=True, vmem_limit_bytes=62 << 20
         ),
         name="exchange",
     )(bags, tables)
@@ -270,6 +263,8 @@
     features, samples = inv.shape
     mixes = compress.shape[0]
     total, width = rows.shape
+    held = rows.size + weight.size + samples * total + 2 * (mixes + samples) * total
+    held += mixes * samples * width + 2 * features * mixes * samples
     vmem = pl.BlockSpec(memory_space=pltpu.VMEM)
     smem = pl.BlockSpec(memory_space=pltpu.SMEM)
     return pl.pallas_call(
@@ -284,7 +279,7 @@
             pltpu.VMEM((mixes * samples, width), BF16),
             pltpu.VMEM((features * mixes, samples), F32),
         ],
-        compiler_params=pltpu.CompilerParams(vmem_limit_bytes=60 << 20),
+        compiler_params=pltpu.CompilerParams(vmem_limit_bytes=min(60 << 20, (8 << 20) + 3 * held)),
         name="interact",
     )(rows, inv, order, counts, compress, weight, bias)
 

time: 52.4 us -> 39.8 us (0.76)
  Pallas kernels: 48.9 us -> 36.9 us
  local copies, waits for them, and re-layouts: 2.36 us -> 1.06 us
  other arithmetic: 0.87 us -> 1.59 us
    pallas_call x1, Pallas kernels: 35.9 us -> 24.7 us  [exchange(): pl.pallas_call(functools.partial(exchange_kernel, n, most), out_shape=jax...]
    unnamed x4 -> x14, local copies, waits for them, and re-layouts: 2.36 us -> 1.06 us
    pallas_call x1, Pallas kernels: 13 us -> 12.1 us  [interact(): pl.pallas_call(interact_kernel, out_shape=jax.ShapeDtypeStruct((samples,...]
    select_n x1, other arithmetic: 0.86 us -> 1.58 us  [shards(): jnp.where(active, bag_rows[0].transpose(1, 2, 0) + local, tabs * vocab)]
where the time goes in v2:
time: 39.8 us; the launch traced here: 39.6 us
  Pallas kernels  36.9 us (93%)
  other arithmetic  1.59 us (4%)
  local copies, waits for them, and re-layouts  1.06 us (3%)
    pallas_call x1, Pallas kernels, exchange(): pl.pallas_call(functools.partial(exchange_kernel, n, most), out_shape=jax...  24.7 us
    pallas_call x1, Pallas kernels, interact(): pl.pallas_call(interact_kernel, out_shape=jax.ShapeDtypeStruct((samples,...  12.1 us
    select_n x1, other arithmetic, shards(): jnp.where(active, bag_rows[0].transpose(1, 2, 0) + local, tabs * vocab)  1.58 us
    unnamed x14, local copies, waits for them, and re-layouts  1.06 us

profile of v2, /device:TPU:0, one launch (start us, length us, event | category | flops | bytes accessed | tf_op | source)
XLA Modules:
  0.0 39.6 jit_solution(3892309151472898840)
XLA Ops:
  0.0 0.0 copy-start.4
  0.0 0.0 copy-start.1
  0.0 0.0 copy-start.3
  0.0 0.0 copy-start.5
  0.0 0.0 copy-start.2
  0.0 0.0 copy-start.6
  0.0 1.6 %bitcast_select_fusion = s32[32,4,64]{2,1,0:T(4,128)} fusion(s32[1,64,32,4]{1,3,2,0:T(4,128)} %param.10, s32[64]{0:T(128)S(1)} %fusion, s32[32,64]{1,0:T(8,128)} %bitcast.19), kind=kLoop, calls=%fused_computation | loop fusion | flops 24576 | bytes 73984 | tf_op jit(solution)/shard_map/jit(_where)/select_n | solution.py:294
  1.6 24.7 %exchange.1 = bf16[16,128,128]{2,1,0:T(8,128)(2,1)} custom-call(s32[128,64]{1,0:T(8,128)} %bitcast.18, bf16[4,2048,128]{2,1,0:T(8,128)(2,1)} %tables_ref.1), custom_call_target="tpu_custom_call" | custom-call | tf_op jit(solution)/shard_map/exchange/pallas_call | solution.py:140
  26.3 0.0 copy-done.4
  26.3 0.0 copy-done.1
  26.4 0.0 copy-done.3
  26.4 0.0 copy-done.5
  26.4 0.0 copy-done.2
  26.4 0.0 copy-done.6
  26.4 0.0 copy-start
  26.4 1.0 %copy-done = bf16[16,128,128]{2,1,0:T(8,128)(2,1)S(1)} copy-done((bf16[16,128,128]{2,1,0:T(8,128)(2,1)S(1)}, bf16[16,128,128]{2,1,0:T(8,128)(2,1)}, u32[]{:S(2)}) %copy-start) | copy-done | bytes 524312
  27.4 12.1 %interact.1 = bf16[128,512]{1,0:T(8,128)(2,1)} custom-call(bf16[2048,128]{1,0:T(8,128)(2,1)S(1)} %bitcast.14, s32[64,128]{1,0:T(8,128)S(1)} %bitcast.15, s32[64]{0:T(128)S(1)} %copy-done.5, s32[64]{0:T(128)S(1)} %bitcast.17, bf16[16,64]{1,0:T(8,128)(2,1)S(1)} %copy-done.3, bf16[1024,512]{1,0:T(8,128)(2,1)S(1)} %copy-done.1, f32[1,512]{1,0:T(1,128)S(1)} %bitcast.16), custom_call_target="tpu_custom_call" | custom-call | tf_op jit(solution)/shard_map/interact/pallas_call | solution.py:270
  (1 shorter events, 0.0 us)
Async XLA Ops:
  0.0 26.3 %copy-start.4 = (f32[512]{0:T(512)S(1)}, f32[512]{0:T(512)}, u32[]{:S(2)}) copy-start(f32[512]{0:T(512)} %param.17) | copy-start | bytes 6148
  0.0 26.3 %copy-start.1 = (bf16[1024,512]{1,0:T(8,128)(2,1)S(1)}, bf16[1024,512]{1,0:T(8,128)(2,1)}, u32[]{:S(2)}) copy-start(bf16[1024,512]{1,0:T(8,128)(2,1)} %weight_ref.1) | copy-start | bytes 3145732
  0.0 26.4 %copy-start.3 = (bf16[16,64]{1,0:T(8,128)(2,1)S(1)}, bf16[16,64]{1,0:T(8,128)(2,1)}, u32[]{:S(2)}) copy-start(bf16[16,64]{1,0:T(8,128)(2,1)} %compress_ref.1) | copy-start | bytes 6148
  0.0 26.4 %copy-start.5 = (s32[64]{0:T(128)S(1)}, s32[64]{0:T(128)}, u32[]{:S(2)}) copy-start(s32[64]{0:T(128)} %order_ref.1) | copy-start | bytes 772
  0.0 26.4 %copy-start.2 = (s32[128,64]{0,1:T(8,128)S(1)}, s32[128,64]{0,1:T(8,128)}, u32[]{:S(2)}) copy-start(s32[128,64]{0,1:T(8,128)} %param.13) | copy-start | bytes 98308
  0.0 26.4 %copy-start.6 = (s32[1,64]{1,0:T(1,128)S(1)}, s32[1,64]{1,0:T(1,128)}, u32[]{:S(2)}) copy-start(s32[1,64]{1,0:T(1,128)} %param.12) | copy-start | bytes 772
  26.4 1.0 %copy-start = (bf16[16,128,128]{2,1,0:T(8,128)(2,1)S(1)}, bf16[16,128,128]{2,1,0:T(8,128)(2,1)}, u32[]{:S(2)}) copy-start(bf16[16,128,128]{2,1,0:T(8,128)(2,1)} %exchange.1) | copy-start | bytes 1572868

commit v3 on v2

v3 whole, which is shorter than its diff:
```python
import functools

import jax
import jax.numpy as jnp
from jax import lax
from jax.experimental import pallas as pl
from jax.experimental.pallas import tpu as pltpu
from jax.sharding import PartitionSpec as P

F32 = jnp.float32
BF16 = jnp.bfloat16


def select_samples(
    most, inv_ref, order_ref, counts_ref, compress_ref, sel, spread_c, mask
):
    features, samples = inv_ref.shape
    per = 8
    span = per * most
    inv = inv_ref[...].astype(F32).T.astype(BF16)
    comp = compress_ref[...]

    def select(c, carry):
        lane = lax.broadcasted_iota(jnp.int32, (1, span), 1)
        slot, unit = lane // most, lane % most
        order_row = jnp.zeros((1, span), jnp.int32)
        count_row = jnp.zeros((1, span), jnp.int32)
        row_u = lax.broadcasted_iota(jnp.int32, (most, samples), 0)
        for i in range(per):
            s = c * per + i
            f, count = order_ref[s], counts_ref[s]
            order_row = jnp.where(slot == i, f, order_row)
            count_row = jnp.where(slot == i, count, count_row)
            wanted = inv_ref[pl.ds(f, 1), :]
            hit = jnp.logical_and(row_u == wanted, row_u < count)
            mask[pl.ds(pl.multiple_of(s * most, most), most), :] = jnp.where(hit, 1.0, 0.0)
        target = jnp.where(unit < count_row, unit, -1).astype(F32)
        feature = lax.broadcasted_iota(jnp.int32, (features, span), 0)
        one_hot = jnp.where(feature == order_row, 1.0, 0.0).astype(BF16)
        inv_all = jnp.dot(inv, one_hot, preferred_element_type=F32)
        columns = pl.ds(pl.multiple_of(c * span, span), span)
        sel[:, columns] = jnp.where(inv_all == target, 1.0, 0.0).astype(BF16)
        spread_c[:, columns] = jnp.dot(comp, one_hot, preferred_element_type=F32)
        return carry

    lax.fori_loop(0, features // per, select, 0)


def exchange_kernel(
    n, most, bags_ref, tables_ref, inv_ref, order_ref, counts_ref, compress_ref,
    rows_ref, sel, spread_c, mask,
    tab16, tab32, ids_out, ids_in, pooled, staging,
    tab_sem, id_send, id_recv, smem_sem, row_send, row_recv,
):
    me = lax.axis_index("dev")
    tabs, vocab, width = tables_ref.shape
    spread = bags_ref.shape[0]
    pooling = spread // most
    zero_row = tabs * vocab

    table_copy = pltpu.make_async_copy(tables_ref, tab16, tab_sem)
    table_copy.start()
    barrier = pltpu.get_barrier_semaphore()

    def greet(i, carry):
        pl.semaphore_signal(barrier, inc=1, device_id={"dev": lax.rem(me + i, n)})
        return carry

    lax.fori_loop(1, n, greet, 0)

    index = bags_ref[...].T
    for g in range(n):
        ids_out[g] = index[g * tabs:(g + 1) * tabs]

    pl.semaphore_wait(barrier, n - 1)

    def id_copy(i):
        peer = lax.rem(me + i, n)
        return pltpu.make_async_remote_copy(
            src_ref=ids_out.at[peer], dst_ref=ids_in.at[me],
            send_sem=id_send.at[peer], recv_sem=id_recv.at[me],
            device_id={"dev": peer},
        )

    def id_arrival(source):
        return pltpu.make_async_remote_copy(
            src_ref=ids_out.at[source], dst_ref=ids_in.at[source],
            send_sem=id_send.at[source], recv_sem=id_recv.at[source],
            device_id={"dev": source},
        )

    def offset(j):
        half = (j + 1) // 2
        return n // 2 + jnp.where(j % 2 == 1, half, -half)

    def send_ids(j, carry):
        id_copy(offset(j)).start()
        return carry

    lax.fori_loop(0, n - 1, send_ids, 0)

    own_ids = pltpu.make_async_copy(ids_out.at[me], ids_in.at[me], smem_sem)
    own_ids.start()
    table_copy.wait()
    tab32[pl.ds(zero_row, 8), :] = jnp.zeros((8, width), F32)
    step = 256

    def widen(i, carry):
        for t in range(tabs):
            base = pl.multiple_of(i * step, step)
            tab32[pl.ds(t * vocab + base, step), :] = tab16[t, pl.ds(base, step), :].astype(F32)
        return carry

    lax.fori_loop(0, vocab // step, widen, 0)

    def pool(source, store):
        def one_table(t, carry):
            at_table = pl.multiple_of(t * most, most)
            for r in range(most):
                total = None
                for p in range(pooling):
                    row = tab32[pl.ds(ids_in[source, t, r * pooling + p], 1), :]
                    total = row if total is None else total + row
                pooled[pl.ds(at_table + r, 1), :] = total
            return carry

        lax.fori_loop(0, tabs, one_table, 0)
        store(pooled[...].astype(BF16))

    def row_copy(peer):
        return pltpu.make_async_remote_copy(
            src_ref=staging.at[peer], dst_ref=rows_ref.at[me],
            send_sem=row_send.at[peer], recv_sem=row_recv.at[me],
            device_id={"dev": peer},
        )

    def serve(j, carry):
        peer = lax.rem(me + offset(j), n)
        id_arrival(peer).wait_recv()

        def store(value):
            staging[peer] = value

        pool(peer, store)
        row_copy(peer).start()
        return carry

    lax.fori_loop(0, n - 1, serve, 0)

    own_ids.wait()

    def store_own(value):
        rows_ref[me] = value

    pool(me, store_own)
    select_samples(most, inv_ref, order_ref, counts_ref, compress_ref, sel, spread_c, mask)

    def finish(i, carry):
        peer = lax.rem(me + i, n)
        id_copy(i).wait_send()
        row_copy(peer).wait_send()
        pltpu.make_async_remote_copy(
            src_ref=staging.at[peer], dst_ref=rows_ref.at[peer],
            send_sem=row_send.at[peer], recv_sem=row_recv.at[peer],
            device_id={"dev": peer},
        ).wait_recv()
        return carry

    lax.fori_loop(1, n, finish, 0)


def exchange(n, most, bags, tables, inv, order, counts, compress):
    tabs, vocab, width = tables.shape
    spread, slots = bags.shape
    block = tabs * most
    total, samples, mixes = n * block, inv.shape[1], compress.shape[0]
    vmem = pl.BlockSpec(memory_space=pltpu.VMEM)
    smem = pl.BlockSpec(memory_space=pltpu.SMEM)
    return pl.pallas_call(
        functools.partial(exchange_kernel, n, most),
        out_shape=[
            jax.ShapeDtypeStruct((n, block, width), BF16),
            jax.ShapeDtypeStruct((samples, total), BF16),
            jax.ShapeDtypeStruct((mixes, total), F32),
            jax.ShapeDtypeStruct((total, samples), F32),
        ],
        in_specs=[vmem, pl.BlockSpec(memory_space=pl.ANY), vmem, smem, smem, vmem],
        out_specs=[vmem] * 4,
        scratch_shapes=[
            pltpu.VMEM(tables.shape, BF16),
            pltpu.VMEM((tabs * vocab + 8, width), F32),
            pltpu.VMEM((n, tabs, spread), jnp.int32),
            pltpu.SMEM((n, tabs, spread), jnp.int32),
            pltpu.VMEM((block, width), F32),
            pltpu.VMEM((n, block, width), BF16),
            pltpu.SemaphoreType.DMA,
            pltpu.SemaphoreType.DMA((n,)),
            pltpu.SemaphoreType.DMA((n,)),
            pltpu.SemaphoreType.DMA,
            pltpu.SemaphoreType.DMA((n,)),
            pltpu.SemaphoreType.DMA((n,)),
        ],
        compiler_params=pltpu.CompilerParams(
            collective_id=0, has_side_effects=True, vmem_limit_bytes=50 << 20
        ),
        name="exchange",
    )(bags, tables, inv, order, counts, compress)


def interact_kernel(
    rows_ref, sel, spread_c, mask, order_ref, weight_ref, bias_ref, out_ref, mixed, pairs,
):
    mixes, total = spread_c.shape
    samples = mask.shape[1]
    width = rows_ref.shape[1]
    features = order_ref.shape[0]
    most = total // features
    per = 8
    span = per * most
    deep = min(total, 2048)

    def mix(k, carry):
        acc = jnp.zeros((samples, width), F32)

        def part(q, acc):
            columns = pl.ds(pl.multiple_of(q * deep, deep), deep)
            scaled = sel[:, columns] * spread_c[pl.ds(k, 1), columns].astype(BF16)
            return acc + jnp.dot(scaled, rows_ref[columns, :], preferred_element_type=F32)

        if total == deep:
            acc = part(0, acc)
        else:
            acc = lax.fori_loop(0, total // deep, part, acc)
        mixed[pl.ds(pl.multiple_of(k * samples, samples), samples), :] = acc.astype(BF16)
        return carry

    lax.fori_loop(0, mixes, mix, 0)

    pair = 2

    def inner(j, carry):
        c8, kp = j // (mixes // pair), j % (mixes // pair)
        wanted = mixed[pl.ds(pl.multiple_of(kp * pair * samples, samples), pair * samples), :]
        for i in range(per):
            c = c8 * per + i
            at = pl.ds(pl.multiple_of(c * span, span), span)
            product = lax.dot_general(
                rows_ref[at, :], wanted, (((1,), (1,)), ((), ())), preferred_element_type=F32
            )
            chosen = mask[at, :]
            for h in range(pair):
                kept = product[:, h * samples:(h + 1) * samples] * chosen
                summed = jnp.sum(kept.reshape(per, most, samples), axis=1)
                for s in range(per):
                    f = order_ref[c * per + s]
                    pairs[pl.ds(f * mixes + kp * pair + h, 1), :] = summed[s:s + 1, :]
        return carry

    lax.fori_loop(0, features // (per * per) * (mixes // pair), inner, 0)

    depth = min(features * mixes, 1024)
    hidden = jnp.zeros(out_ref.shape, F32) + bias_ref[...]

    def top(q, hidden):
        at = pl.ds(pl.multiple_of(q * depth, depth), depth)
        return hidden + lax.dot_general(
            pairs[at, :].astype(BF16), weight_ref[at, :], (((0,), (0,)), ((), ())),
            preferred_element_type=F32,
        )

    if depth == features * mixes:
        hidden = top(0, hidden)
    else:
        hidden = lax.fori_loop(0, features * mixes // depth, top, hidden)
    out_ref[...] = jnp.maximum(hidden, 0.0).astype(BF16)


def interact(rows, sel, spread_c, mask, order, weight, bias):
    mixes, total = spread_c.shape
    samples, features, width = mask.shape[1], order.shape[0], rows.shape[1]
    held = rows.size + weight.size + samples * total + 2 * (mixes + samples) * total
    held += mixes * samples * width + 2 * features * mixes * samples
    vmem = pl.BlockSpec(memory_space=pltpu.VMEM)
    smem = pl.BlockSpec(memory_space=pltpu.SMEM)
    return pl.pallas_call(
        interact_kernel,
        out_shape=jax.ShapeDtypeStruct((samples, weight.shape[1]), BF16),
        in_specs=[vmem, vmem, vmem, vmem, smem, vmem, vmem],
        out_specs=vmem,
        scratch_shapes=[
            pltpu.VMEM((mixes * samples, width), BF16),
            pltpu.VMEM((features * mixes, samples), F32),
        ],
        compiler_params=pltpu.CompilerParams(vmem_limit_bytes=min(60 << 20, (8 << 20) + 3 * held)),
        name="interact",
    )(rows, sel, spread_c, mask, order, weight, bias)


def shards(
    n, tables, bag_rows, bag_lengths, row_counts, inverse, table_order, compress, top_weight, top_bias
):
    _, slots, most, pooling = bag_rows.shape
    tabs, vocab, width = tables.shape
    local = (jnp.arange(slots, dtype=jnp.int32) % tabs) * vocab
    active = jnp.arange(pooling, dtype=jnp.int32)[:, None] < bag_lengths[0].T[:, None, :]
    index = jnp.where(active, bag_rows[0].transpose(1, 2, 0) + local, tabs * vocab)
    rows, sel, spread_c, mask = exchange(
        n, most, index.reshape(most * pooling, slots), tables,
        inverse.T, table_order, row_counts[0], compress,
    )
    return interact(
        rows.reshape(slots * most, width), sel, spread_c, mask, table_order,
        top_weight, top_bias.reshape(1, -1),
    )


def solution(mesh):
    return jax.shard_map(
        functools.partial(shards, mesh.shape["dev"]),
        mesh=mesh,
        in_specs=(
            P("dev", None, None),
            P(("rep", "dev"), None, None, None),
            P(("rep", "dev"), None, None),
            P(("rep", "dev"), None),
            P(("rep", "dev"), None),
            P(),
            P(),
            P(),
            P(),
        ),
        out_specs=P(("rep", "dev"), None),
        check_vma=False,
    )
```

time: 39.8 us -> 38.3 us (0.962)
  Pallas kernels: 36.9 us -> 34.3 us
  local copies, waits for them, and re-layouts: 1.06 us -> 2.76 us
  other arithmetic: 1.59 us -> 0.96 us
    unnamed x14 -> x12, local copies, waits for them, and re-layouts: 1.06 us -> 2.76 us
    pallas_call x1, Pallas kernels: 12.1 us -> 10.6 us  [interact(): pl.pallas_call(interact_kernel, out_shape=jax.ShapeDtypeStruct((samples,...]
    pallas_call x1, Pallas kernels: 24.7 us -> 23.7 us  [exchange(): pl.pallas_call(functools.partial(exchange_kernel, n, most), out_shape=[ja...]
    select_n x1, other arithmetic: 1.58 us -> 0.95 us  [shards(): jnp.where(active, bag_rows[0].transpose(1, 2, 0) + local, tabs * vocab)]
where the time goes in v3:
time: 38.3 us; the launch traced here: 38.1 us
  Pallas kernels  34.3 us (90%)
  local copies, waits for them, and re-layouts  2.76 us (7%)
  other arithmetic  0.96 us (3%)
    pallas_call x1, Pallas kernels, exchange(): pl.pallas_call(functools.partial(exchange_kernel, n, most), out_shape=[ja...  23.7 us
    pallas_call x1, Pallas kernels, interact(): pl.pallas_call(interact_kernel, out_shape=jax.ShapeDtypeStruct((samples,...  10.6 us
    unnamed x12, local copies, waits for them, and re-layouts  2.76 us
    select_n x1, other arithmetic, shards(): jnp.where(active, bag_rows[0].transpose(1, 2, 0) + local, tabs * vocab)  0.95 us

profile of v3, /device:TPU:0, one launch (start us, length us, event | category | flops | bytes accessed | tf_op | source)
XLA Modules:
  0.0 38.1 jit_solution(14524661708482330341)
XLA Ops:
  0.0 0.0 copy-start
  0.0 1.0 %bitcast_select_fusion = s32[32,4,64]{2,1,0:T(4,128)S(1)} fusion(s32[1,64,32,4]{1,3,2,0:T(4,128)} %param.10, s32[64]{0:T(128)S(1)} %fusion, s32[32,64]{1,0:T(8,128)} %bitcast.19), kind=kLoop, calls=%fused_computation | loop fusion | flops 24576 | bytes 73984 | tf_op jit(solution)/shard_map/jit(_where)/select_n | solution.py:306
  1.0 0.0 copy-start.1
  1.0 0.7 %copy-done.1 = s32[128,64]{0,1:T(8,128)S(1)} copy-done((s32[128,64]{0,1:T(8,128)S(1)}, s32[128,64]{0,1:T(8,128)}, u32[]{:S(2)}) %copy-start.1) | copy-done | bytes 32792
  1.7 0.0 copy-start.2
  1.7 0.7 %copy-done.2 = bf16[16,64]{1,0:T(8,128)(2,1)S(1)} copy-done((bf16[16,64]{1,0:T(8,128)(2,1)S(1)}, bf16[16,64]{1,0:T(8,128)(2,1)}, u32[]{:S(2)}) %copy-start.2) | copy-done | bytes 2072
  2.4 0.0 copy-start.4
  2.4 0.7 %copy-done.4 = s32[64]{0:T(128)S(1)} copy-done((s32[64]{0:T(128)S(1)}, s32[64]{0:T(128)}, u32[]{:S(2)}) %copy-start.4) | copy-done | bytes 280
  3.1 0.0 copy-start.5
  3.1 0.7 %copy-done.5 = s32[1,64]{1,0:T(1,128)S(1)} copy-done((s32[1,64]{1,0:T(1,128)S(1)}, s32[1,64]{1,0:T(1,128)}, u32[]{:S(2)}) %copy-start.5) | copy-done | bytes 280
  3.7 0.0 copy-start.3
  3.7 23.7 %exchange.1 = (bf16[16,128,128]{2,1,0:T(8,128)(2,1)S(1)}, bf16[128,2048]{1,0:T(8,128)(2,1)S(1)}, f32[16,2048]{1,0:T(8,128)S(1)}, f32[2048,128]{1,0:T(8,128)S(1)}) custom-call(s32[128,64]{1,0:T(8,128)S(1)} %bitcast.15, bf16[4,2048,128]{2,1,0:T(8,128)(2,1)} %tables_ref.1, s32[64,128]{1,0:T(8,128)S(1)} %bitcast.16, s32[64]{0:T(128)S(1)} %copy-done.4, ...), custom_call_target="tpu_custom_call" | custom-call | tf_op jit(solution)/shard_map/exchange/pallas_call | solution.py:179
  27.5 0.0 copy-done
  27.5 0.0 copy-done.3
  27.5 10.6 %interact.1 = bf16[128,512]{1,0:T(8,128)(2,1)} custom-call(bf16[2048,128]{1,0:T(8,128)(2,1)S(1)} %bitcast.14, bf16[128,2048]{1,0:T(8,128)(2,1)S(1)} %get-tuple-element.10.sel, f32[16,2048]{1,0:T(8,128)S(1)} %get-tuple-element.11.spread_c, f32[2048,128]{1,0:T(8,128)S(1)} %get-tuple-element.12.mask, s32[64]{0:T(128)S(1)} %copy-done.4, ...), custom_call_target="tpu_custom_call" | custom-call | tf_op jit(solution)/shard_map/interact/pallas_call | solution.py:285
  (1 shorter events, 0.0 us)
Async XLA Ops:
  0.0 27.5 %copy-start = (bf16[1024,512]{1,0:T(8,128)(2,1)S(1)}, bf16[1024,512]{1,0:T(8,128)(2,1)}, u32[]{:S(2)}) copy-start(bf16[1024,512]{1,0:T(8,128)(2,1)} %weight_ref.1) | copy-start | bytes 3145732
  1.0 0.8 %copy-start.1 = (s32[128,64]{0,1:T(8,128)S(1)}, s32[128,64]{0,1:T(8,128)}, u32[]{:S(2)}) copy-start(s32[128,64]{0,1:T(8,128)} %param.13) | copy-start | bytes 98308
  1.7 0.7 %copy-start.2 = (bf16[16,64]{1,0:T(8,128)(2,1)S(1)}, bf16[16,64]{1,0:T(8,128)(2,1)}, u32[]{:S(2)}) copy-start(bf16[16,64]{1,0:T(8,128)(2,1)} %compress_ref.1) | copy-start | bytes 6148
  2.4 0.7 %copy-start.4 = (s32[64]{0:T(128)S(1)}, s32[64]{0:T(128)}, u32[]{:S(2)}) copy-start(s32[64]{0:T(128)} %order_ref.3) | copy-start | bytes 772
  3.1 0.7 %copy-start.5 = (s32[1,64]{1,0:T(1,128)S(1)}, s32[1,64]{1,0:T(1,128)}, u32[]{:S(2)}) copy-start(s32[1,64]{1,0:T(1,128)} %param.12) | copy-start | bytes 772
  3.7 23.7 %copy-start.3 = (f32[512]{0:T(512)S(1)}, f32[512]{0:T(512)}, u32[]{:S(2)}) copy-start(f32[512]{0:T(512)} %param.17) | copy-start | bytes 6148
